TPU v7x, 32 devices: a whole 2x2x4 slice. The times are simulated.
32 devices in a mesh: blk: 16 (over z, y, core), rows: 2 (over x).
Axes of the slice: x: 2, y: 2, z: 4, core: 2. Of those that a mesh axis runs over, the one named last changes fastest.
Arguments:
- columns: float32 [2048, 1280], P('blk', 'rows'), may hold values from -9 to 9
- right_factor: float32 [2048, 512], P('blk', 'rows'), may hold values from -6 to 6
Outputs:
- new_columns: float32 [2048, 1280], P('blk', 'rows')
- new_factor: float32 [2048, 512], P('blk', 'rows')
All inputs are finite; a program needn't handle non-finite values.
Results may differ from a plain program's by a relative error of at most 0.0003.
Values sent between devices are 32-bit elements; how exact they have to be, the bound alone decides.
A program may use at most 64 MiB of HBM per device.

v0:
```python
import jax
import jax.numpy as jnp
from jax import lax
from jax.experimental import pallas as pl
from jax.experimental.pallas import tpu as pltpu
from jax.sharding import PartitionSpec as P

STEPS = 6
PANEL = 16
LANES = 128
MESH = pl.DeviceIdType.MESH

HIGHEST_PREC = lax.Precision.HIGHEST


def dot_nn(a, b):
    return lax.dot_general(
        a, b, (((1,), (0,)), ((), ())), precision=HIGHEST_PREC, preferred_element_type=jnp.float32
    )


def dot_nt(a, b):
    return lax.dot_general(
        a, b, (((1,), (1,)), ((), ())), precision=HIGHEST_PREC, preferred_element_type=jnp.float32
    )


def dot_tn(a, b):
    return lax.dot_general(
        a, b, (((0,), (0,)), ((), ())), precision=HIGHEST_PREC, preferred_element_type=jnp.float32
    )


def eliminate(work, midway=None):
    order, width = work.shape
    panels = order // PANEL
    for panel in range(panels):
        if midway is not None and panel == panels // 2 - 1:
            midway()
        low = panel * PANEL
        high = low + PANEL
        end = min(high + PANEL, order)
        rows = work[low:high, :]
        below = work[high:end, :] if end > high else None
        spread = [
            jnp.broadcast_to(rows[:, low + k : low + k + 1], (PANEL, 128)) for k in range(PANEL)
        ]
        spread_below = None
        if below is not None:
            spread_below = [
                jnp.broadcast_to(below[:, low + k : low + k + 1], (end - high, 128))
                for k in range(PANEL)
            ]
        done = []
        for j in range(PANEL):
            scale = lax.rsqrt(spread[j][j : j + 1, :])
            column = spread[j] * scale
            wide = jnp.concatenate([scale] * (width // 128), axis=1)
            pivot_row = rows[j : j + 1, :] * wide
            done.append(pivot_row)
            wide_column = jnp.concatenate([column] * (width // 128), axis=1)
            if j + 1 < PANEL:
                rows = rows - wide_column * pivot_row
            if below is not None:
                column_below = spread_below[j] * scale
                wide_below = jnp.concatenate([column_below] * (width // 128), axis=1)
                below = below - wide_below * pivot_row
            for k in range(j + 1, PANEL):
                head = spread[k][j : j + 1, :] * scale
                spread[k] = spread[k] - column * head
                if below is not None:
                    spread_below[k] = spread_below[k] - column_below * head
        finished = jnp.concatenate(done, axis=0)
        work[low:high, :] = finished
        if below is not None:
            work[high:end, :] = below
        if end < order:
            work[end:, :] = work[end:, :] - dot_tn(finished[:, end:order], finished)


def lanes(chunk):
    return slice(chunk * LANES, (chunk + 1) * LANES)


def cycle_kernel(
    columns, right_factor, new_columns, new_factor, own, near, stay_fac, sent_fac, held_fac, grams,
    near_grams, lows, near_lows, cross, work, solve, pair_sent, pair_sem, fac_sent, fac_sem, gram_sent,
    gram_sem, low_sent, low_sem, cross_sent, cross_sem,
):
    half = columns.shape[0] // 2
    order = 2 * half
    col_chunks = columns.shape[1] // LANES
    fac_chunks = right_factor.shape[1] // LANES
    ring, peers = lax.axis_size("blk"), lax.axis_size("rows")
    place, row_place = lax.axis_index("blk"), lax.axis_index("rows")
    right, left = lax.rem(place + 1, ring), lax.rem(place + ring - 1, ring)

    barrier = pltpu.get_barrier_semaphore()
    for neighbour in (left, right):
        pl.semaphore_signal(barrier, inc=1, device_id={"blk": neighbour}, device_id_type=MESH)
    for off in range(1, peers):
        peer = lax.rem(row_place + off, peers)
        pl.semaphore_signal(barrier, inc=1, device_id={"rows": peer}, device_id_type=MESH)

    def to_right(source, target, send_sem, recv_sem):
        return pltpu.make_async_remote_copy(
            src_ref=source,
            dst_ref=target,
            send_sem=send_sem,
            recv_sem=recv_sem,
            device_id={"blk": right},
            device_id_type=MESH,
        )

    def pair_copy(step, chunk):
        return to_right(
            own.at[step, chunk], near.at[step, chunk], pair_sent.at[step, chunk], pair_sem.at[step, chunk]
        )

    def fac_copy(step, chunk):
        return to_right(
            sent_fac.at[step, chunk],
            held_fac.at[step + 1, chunk],
            fac_sent.at[step, chunk],
            fac_sem.at[step, chunk],
        )

    def gram_copy(step):
        return to_right(grams.at[step], near_grams.at[step], gram_sent.at[step], gram_sem.at[step])

    def low_copy(step):
        return to_right(lows.at[step], near_lows.at[step], low_sent.at[step], low_sem.at[step])

    def cross_copy(slot, off):
        part = cross.at[slot, row_place]
        return pltpu.make_async_remote_copy(
            src_ref=part,
            dst_ref=part,
            send_sem=cross_sent.at[slot, off - 1],
            recv_sem=cross_sem.at[slot, off - 1],
            device_id={"rows": lax.rem(row_place + off, peers)},
            device_id_type=MESH,
        )

    def cross_sum(slot):
        total = cross[slot, 0]
        for peer in range(1, peers):
            total = total + cross[slot, peer]
        return total

    total = jnp.zeros((order, order), jnp.float32)
    for chunk in range(col_chunks):
        part = columns[:, lanes(chunk)]
        own[0, chunk] = part
        total = total + dot_nt(part, part)
    cross[0, row_place] = total
    for chunk in range(fac_chunks):
        stay_fac[chunk] = right_factor[:half, lanes(chunk)]
        held_fac[0, chunk] = right_factor[half:, lanes(chunk)]
    pl.semaphore_wait(barrier, 2 + peers - 1)
    for off in range(1, peers):
        cross_copy(0, off).start()
    for chunk in range(col_chunks):
        pair_copy(0, chunk).start()
    for off in range(1, peers):
        cross_copy(0, off).wait()
    grams[0] = cross_sum(0)

    def advance(step, carry):
        gram_copy(step).start()
        g = grams[step]
        work[...] = dot_nn(g, g)
        eliminate(work)
        upper = work[...]
        keep = lax.broadcasted_iota(jnp.int32, upper.shape, 0) <= lax.broadcasted_iota(
            jnp.int32, upper.shape, 1
        )
        upper = jnp.where(keep, upper, 0.0)
        solve[:, :order] = dot_nt(upper, upper)
        solve[:, order:] = upper

        def products():
            for chunk in range(col_chunks):
                pair_copy(step, chunk).wait_recv()

            @pl.when(step < STEPS - 1)
            def _():
                total = jnp.zeros((order, order), jnp.float32)
                for chunk in range(col_chunks):
                    total = total + dot_nt(own[step, chunk], near[step, chunk])
                cross[step + 1, row_place] = total
                for off in range(1, peers):
                    cross_copy(step + 1, off).start()

        eliminate(solve, products)
        turn = solve[:, order:]
        top, low = turn[:half], turn[half:]
        lows[step] = low
        low_copy(step).start()

        for chunk in range(col_chunks):
            own[step + 1, chunk, :half] = dot_nn(top, own[step, chunk])

        @pl.when(step > 0)
        def _():
            for chunk in range(fac_chunks):
                fac_copy(step - 1, chunk).wait_recv()

        for chunk in range(fac_chunks):
            turned = dot_nn(turn, jnp.concatenate([stay_fac[chunk], held_fac[step, chunk]], axis=0))
            stay_fac[chunk] = turned[:half]
            sent_fac[step, chunk] = turned[half:]
            fac_copy(step, chunk).start()
        gram_copy(step).wait_recv()

        @pl.when(step < STEPS - 1)
        def _():
            grams[step + 1, :half, :half] = dot_nt(dot_nn(top, grams[step]), top)
            for off in range(1, peers):
                cross_copy(step + 1, off).wait()
            reach = dot_nn(top, cross_sum(step + 1))
            low_copy(step).wait_recv()
            arrived = near_lows[step]
            term = dot_nt(reach, arrived)
            grams[step + 1, :half, half:] = term
            grams[step + 1, half:, :half] = term.T
            grams[step + 1, half:, half:] = dot_nt(dot_nn(arrived, near_grams[step]), arrived)
            for chunk in range(col_chunks):
                own[step + 1, chunk, half:] = dot_nn(arrived, near[step, chunk])
                pair_copy(step + 1, chunk).start()

        for chunk in range(col_chunks):
            pair_copy(step, chunk).wait_send()
        for chunk in range(fac_chunks):
            fac_copy(step, chunk).wait_send()
        gram_copy(step).wait_send()
        low_copy(step).wait_send()
        return carry

    lax.fori_loop(0, STEPS, advance, 0)
    low_copy(STEPS - 1).wait_recv()
    for chunk in range(col_chunks):
        new_columns[:half, lanes(chunk)] = own[STEPS, chunk, :half]
        new_columns[half:, lanes(chunk)] = dot_nn(near_lows[STEPS - 1], near[STEPS - 1, chunk])
    for chunk in range(fac_chunks):
        fac_copy(STEPS - 1, chunk).wait_recv()
        new_factor[:half, lanes(chunk)] = stay_fac[chunk]
        new_factor[half:, lanes(chunk)] = held_fac[STEPS, chunk]


def body(columns, right_factor):
    order = columns.shape[0]
    half = order // 2
    col_chunks = columns.shape[1] // LANES
    fac_chunks = right_factor.shape[1] // LANES
    peers = lax.axis_size("rows")

    def room(*shape):
        return pltpu.VMEM(shape, jnp.float32)

    return pl.pallas_call(
        cycle_kernel,
        out_shape=[jax.ShapeDtypeStruct(a.shape, a.dtype) for a in (columns, right_factor)],
        in_specs=[pl.BlockSpec(memory_space=pltpu.VMEM)] * 2,
        out_specs=[pl.BlockSpec(memory_space=pltpu.VMEM)] * 2,
        scratch_shapes=[
            room(STEPS + 1, col_chunks, order, LANES),
            room(STEPS, col_chunks, order, LANES),
            room(fac_chunks, half, LANES),
            room(STEPS, fac_chunks, half, LANES),
            room(STEPS + 1, fac_chunks, half, LANES),
            room(STEPS, order, order),
            room(STEPS, order, order),
            room(STEPS, half, order),
            room(STEPS, half, order),
            room(STEPS, peers, order, order),
            room(order, order),
            room(order, 2 * order),
            pltpu.SemaphoreType.DMA((STEPS, col_chunks)),
            pltpu.SemaphoreType.DMA((STEPS, col_chunks)),
            pltpu.SemaphoreType.DMA((STEPS, fac_chunks)),
            pltpu.SemaphoreType.DMA((STEPS, fac_chunks)),
            pltpu.SemaphoreType.DMA((STEPS,)),
            pltpu.SemaphoreType.DMA((STEPS,)),
            pltpu.SemaphoreType.DMA((STEPS,)),
            pltpu.SemaphoreType.DMA((STEPS,)),
            pltpu.SemaphoreType.DMA((STEPS, peers - 1)),
            pltpu.SemaphoreType.DMA((STEPS, peers - 1)),
        ],
        compiler_params=pltpu.CompilerParams(collective_id=0, has_side_effects=True),
        name="cycle",
    )(columns, right_factor)


def solution(mesh):
    return jax.shard_map(
        body,
        mesh=mesh,
        in_specs=(P("blk", "rows"), P("blk", "rows")),
        out_specs=(P("blk", "rows"), P("blk", "rows")),
        check_vma=False,
    )
```

profile of v0, /device:TPU:0, one launch (start us, length us, event | category | flops | bytes accessed | tf_op | source)
XLA Modules:
  0.0 77.2 jit_solution(5254872585689441689)
XLA Ops:
  0.6 74.1 %cycle.1 = (f32[128,640]{1,0:T(8,128)}, f32[128,256]{1,0:T(8,128)}) custom-call(f32[128,640]{1,0:T(8,128)} %columns.1, f32[128,256]{1,0:T(8,128)} %right_factor.1), custom_call_target="tpu_custom_call" | custom-call | tf_op jit(solution)/shard_map/cycle/pallas_call | solution.py:261
  74.7 0.0 copy-start
  74.7 1.8 %copy.6 = f32[128,640]{1,0:T(8,128)} copy(f32[128,640]{1,0:T(8,128)} %get-tuple-element.4) | data formatting | bytes 655360
  76.5 0.0 copy-done
  76.5 0.7 copy.7
Async XLA Ops:
  74.7 1.8 %copy-start = (f32[128,256]{1,0:T(8,128)S(1)}, f32[128,256]{1,0:T(8,128)}, u32[]{:S(2)}) copy-start(f32[128,256]{1,0:T(8,128)} %get-tuple-element.5) | copy-start | bytes 393220
where the time goes:
time: 77.3 us; the launch traced here: 77.2 us
  Pallas kernels  74.1 us (96%)
  local copies, waits for them, and re-layouts  2.41 us (3%)
    pallas_call x1, Pallas kernels, body(): pl.pallas_call(cycle_kernel, out_shape=[jax.ShapeDtypeStruct(a.shape, a.d...  74.1 us
    unnamed x4, local copies, waits for them, and re-layouts  2.41 us

commit v1 on v0

--- a/solution.py
+++ b/solution.py
@@ -78,13 +78,35 @@
             work[end:, :] = work[end:, :] - dot_tn(finished[:, end:order], finished)
 
 
+def grid_of(shape):
+    return lax.broadcasted_iota(jnp.int32, shape, 0), lax.broadcasted_iota(jnp.int32, shape, 1)
+
+
+def trace(square):
+    down, across = grid_of(square.shape)
+    kept = jnp.where(down == across, square, 0.0)
+    return jnp.sum(jnp.sum(kept, axis=0, keepdims=True), axis=1, keepdims=True)
+
+
+def scale_of(total):
+    return jnp.broadcast_to(1.0 / (total * total), (8, LANES))
+
+
+def orthogonal(turn):
+    overlap = dot_nt(turn, turn)
+    down, across = grid_of(overlap.shape)
+    lower = jnp.where(down > across, overlap, 0.0)
+    lower = jnp.where(down == across, 0.5 * (overlap - 1.0), lower)
+    return turn - dot_nn(lower, turn)
+
+
 def lanes(chunk):
     return slice(chunk * LANES, (chunk + 1) * LANES)
 
 
 def cycle_kernel(
     columns, right_factor, new_columns, new_factor, own, near, stay_fac, sent_fac, held_fac, grams,
-    near_grams, lows, near_lows, cross, work, solve, pair_sent, pair_sem, fac_sent, fac_sem, gram_sent,
+    near_grams, lows, near_lows, cross, scale, solve, pair_sent, pair_sem, fac_sent, fac_sem, gram_sent,
     gram_sem, low_sent, low_sem, cross_sent, cross_sem,
 ):
     half = columns.shape[0] // 2
@@ -165,19 +187,14 @@
     for off in range(1, peers):
         cross_copy(0, off).wait()
     grams[0] = cross_sum(0)
+    scale[...] = scale_of(trace(grams[0]))
 
     def advance(step, carry):
         gram_copy(step).start()
         g = grams[step]
-        work[...] = dot_nn(g, g)
-        eliminate(work)
-        upper = work[...]
-        keep = lax.broadcasted_iota(jnp.int32, upper.shape, 0) <= lax.broadcasted_iota(
-            jnp.int32, upper.shape, 1
-        )
-        upper = jnp.where(keep, upper, 0.0)
-        solve[:, :order] = dot_nt(upper, upper)
-        solve[:, order:] = upper
+        square = dot_nn(g, g) * scale[:1, :]
+        solve[:, :order] = dot_nn(square, square)
+        solve[:, order:] = square
 
         def products():
             for chunk in range(col_chunks):
@@ -193,7 +210,7 @@
                     cross_copy(step + 1, off).start()
 
         eliminate(solve, products)
-        turn = solve[:, order:]
+        turn = orthogonal(solve[:, order:])
         top, low = turn[:half], turn[half:]
         lows[step] = low
         low_copy(step).start()
@@ -215,6 +232,7 @@
 
         @pl.when(step < STEPS - 1)
         def _():
+            scale[...] = scale_of(trace(grams[step]) + trace(near_grams[step]))
             grams[step + 1, :half, :half] = dot_nt(dot_nn(top, grams[step]), top)
             for off in range(1, peers):
                 cross_copy(step + 1, off).wait()
@@ -274,7 +292,7 @@
             room(STEPS, half, order),
             room(STEPS, half, order),
             room(STEPS, peers, order, order),
-            room(order, order),
+            room(8, LANES),
             room(order, 2 * order),
             pltpu.SemaphoreType.DMA((STEPS, col_chunks)),
             pltpu.SemaphoreType.DMA((STEPS, col_chunks)),

time: 77.3 us -> 73.4 us (0.950)
  Pallas kernels: 74.1 us -> 70.2 us
    pallas_call x1, Pallas kernels: 74.1 us -> 70.2 us  [body(): pl.pallas_call(cycle_kernel, out_shape=[jax.ShapeDtypeStruct(a.shape, a.d...]
where the time goes in v1:
time: 73.4 us; the launch traced here: 73.3 us
  Pallas kernels  70.2 us (96%)
  local copies, waits for them, and re-layouts  2.41 us (3%)
    pallas_call x1, Pallas kernels, body(): pl.pallas_call(cycle_kernel, out_shape=[jax.ShapeDtypeStruct(a.shape, a.d...  70.2 us
    unnamed x4, local copies, waits for them, and re-layouts  2.41 us

profile of v1, /device:TPU:0, one launch (start us, length us, event | category | flops | bytes accessed | tf_op | source)
XLA Modules:
  0.0 73.3 jit_solution(2004140678519505114)
XLA Ops:
  0.6 70.2 %cycle.1 = (f32[128,640]{1,0:T(8,128)}, f32[128,256]{1,0:T(8,128)}) custom-call(f32[128,640]{1,0:T(8,128)} %columns.1, f32[128,256]{1,0:T(8,128)} %right_factor.1), custom_call_target="tpu_custom_call" | custom-call | tf_op jit(solution)/shard_map/cycle/pallas_call | solution.py:279
  70.9 0.0 copy-start
  70.9 1.8 %copy.6 = f32[128,640]{1,0:T(8,128)} copy(f32[128,640]{1,0:T(8,128)} %get-tuple-element.4) | data formatting | bytes 655360
  72.6 0.0 copy-done
  72.6 0.7 copy.7
Async XLA Ops:
  70.9 1.8 %copy-start = (f32[128,256]{1,0:T(8,128)S(1)}, f32[128,256]{1,0:T(8,128)}, u32[]{:S(2)}) copy-start(f32[128,256]{1,0:T(8,128)} %get-tuple-element.5) | copy-start | bytes 393220

commit v2 on v1

v2 whole, which is shorter than its diff:
```python
import jax
import jax.numpy as jnp
from jax import lax
from jax.experimental import pallas as pl
from jax.experimental.pallas import tpu as pltpu
from jax.sharding import PartitionSpec as P

STEPS = 6
PANEL = 16
LANES = 128
MESH = pl.DeviceIdType.MESH

HIGHEST_PREC = lax.Precision.HIGHEST


def dot_nn(a, b):
    return lax.dot_general(
        a, b, (((1,), (0,)), ((), ())), precision=HIGHEST_PREC, preferred_element_type=jnp.float32
    )


def dot_nt(a, b):
    return lax.dot_general(
        a, b, (((1,), (1,)), ((), ())), precision=HIGHEST_PREC, preferred_element_type=jnp.float32
    )


def dot_tn(a, b):
    return lax.dot_general(
        a, b, (((0,), (0,)), ((), ())), precision=HIGHEST_PREC, preferred_element_type=jnp.float32
    )


def split(a):
    high = a.astype(jnp.bfloat16)
    return high, (a - high.astype(jnp.float32)).astype(jnp.bfloat16)


def split_left(a, axis=1):
    high, low = split(a)
    return jnp.concatenate([high, low, high], axis=axis)


def split_right(b, axis=0):
    high, low = split(b)
    return jnp.concatenate([high, high, low], axis=axis)


def mix(turn, block):
    return lax.dot_general(
        split_left(turn), split_right(block), (((1,), (0,)), ((), ())), preferred_element_type=jnp.float32
    )


def cross_of(a, b):
    return lax.dot_general(
        split_left(a), split_right(b, 1), (((1,), (1,)), ((), ())), preferred_element_type=jnp.float32
    )


def eliminate(work, hooks):
    order, width = work.shape
    panels = order // PANEL
    for panel in range(panels):
        if panel in hooks:
            hooks[panel]()
        low = panel * PANEL
        high = low + PANEL
        end = min(high + PANEL, order)
        rows = work[low:high, :]
        below = work[high:end, :] if end > high else None
        spread = [
            jnp.broadcast_to(rows[:, low + k : low + k + 1], (PANEL, 128)) for k in range(PANEL)
        ]
        spread_below = None
        if below is not None:
            spread_below = [
                jnp.broadcast_to(below[:, low + k : low + k + 1], (end - high, 128))
                for k in range(PANEL)
            ]
        done = []
        for j in range(PANEL):
            scale = lax.rsqrt(spread[j][j : j + 1, :])
            column = spread[j] * scale
            wide = jnp.concatenate([scale] * (width // 128), axis=1)
            pivot_row = rows[j : j + 1, :] * wide
            done.append(pivot_row)
            wide_column = jnp.concatenate([column] * (width // 128), axis=1)
            if j + 1 < PANEL:
                rows = rows - wide_column * pivot_row
            if below is not None:
                column_below = spread_below[j] * scale
                wide_below = jnp.concatenate([column_below] * (width // 128), axis=1)
                below = below - wide_below * pivot_row
            for k in range(j + 1, PANEL):
                head = spread[k][j : j + 1, :] * scale
                spread[k] = spread[k] - column * head
                if below is not None:
                    spread_below[k] = spread_below[k] - column_below * head
        finished = jnp.concatenate(done, axis=0)
        work[low:high, :] = finished
        if below is not None:
            work[high:end, :] = below
        if end < order:
            work[end:, :] = work[end:, :] - dot_tn(finished[:, end:order], finished)


def grid_of(shape):
    return lax.broadcasted_iota(jnp.int32, shape, 0), lax.broadcasted_iota(jnp.int32, shape, 1)


def trace(square):
    down, across = grid_of(square.shape)
    kept = jnp.where(down == across, square, 0.0)
    return jnp.sum(jnp.sum(kept, axis=0, keepdims=True), axis=1, keepdims=True)


def scale_of(total):
    return jnp.broadcast_to(1.0 / (total * total), (8, LANES))


def orthogonal(turn):
    overlap = dot_nt(turn, turn)
    down, across = grid_of(overlap.shape)
    lower = jnp.where(down > across, overlap, 0.0)
    lower = jnp.where(down == across, 0.5 * (overlap - 1.0), lower)
    return turn - dot_nn(lower, turn)


def cycle_kernel(
    columns, right_factor, new_columns, new_factor, stay, moving, near_stay, near_moving, stay_fac, sent_fac,
    held_fac, grams, near_grams, turns, near_turns, first, cross, scale, solve, stay_sent,
    stay_sem, moving_sent, moving_sem, fac_sent, fac_sem, gram_sent, gram_sem, low_sent, low_sem, top_sent,
    top_sem, first_sent, first_sem, cross_sent, cross_sem,
):
    half = columns.shape[0] // 2
    order = 2 * half
    upper, lower, beyond = slice(0, half), slice(half, order), slice(order, order + half)
    square = slice(0, order)
    ring, peers = lax.axis_size("blk"), lax.axis_size("rows")
    place, row_place = lax.axis_index("blk"), lax.axis_index("rows")
    right, left = lax.rem(place + 1, ring), lax.rem(place + ring - 1, ring)

    barrier = pltpu.get_barrier_semaphore()
    for neighbour in (left, right):
        pl.semaphore_signal(barrier, inc=1, device_id={"blk": neighbour}, device_id_type=MESH)
    for off in range(1, peers):
        peer = lax.rem(row_place + off, peers)
        pl.semaphore_signal(barrier, inc=1, device_id={"rows": peer}, device_id_type=MESH)

    def to_right(source, target, send_sem, recv_sem):
        return pltpu.make_async_remote_copy(
            src_ref=source,
            dst_ref=target,
            send_sem=send_sem,
            recv_sem=recv_sem,
            device_id={"blk": right},
            device_id_type=MESH,
        )

    def stay_copy():
        return to_right(stay.at[0], near_stay.at[0], stay_sent, stay_sem)

    def moving_copy(step):
        return to_right(
            moving.at[step], near_moving.at[step], moving_sent.at[step], moving_sem.at[step]
        )

    def fac_copy(step):
        return to_right(
            sent_fac.at[step], held_fac.at[step + 1], fac_sent.at[step], fac_sem.at[step]
        )

    def gram_copy(step):
        return to_right(
            grams.at[step, square], near_grams.at[step], gram_sent.at[step], gram_sem.at[step]
        )

    def low_copy(step):
        return to_right(
            turns.at[step, lower], near_turns.at[step, lower], low_sent.at[step], low_sem.at[step]
        )

    def top_copy(step):
        return to_right(
            turns.at[step, upper], near_turns.at[step, upper], top_sent.at[step], top_sem.at[step]
        )

    def to_peer(part, send_sem, recv_sem, off):
        return pltpu.make_async_remote_copy(
            src_ref=part,
            dst_ref=part,
            send_sem=send_sem.at[off - 1],
            recv_sem=recv_sem.at[off - 1],
            device_id={"rows": lax.rem(row_place + off, peers)},
            device_id_type=MESH,
        )

    def first_copy(slot, off):
        return to_peer(first.at[slot, row_place], first_sent.at[slot], first_sem.at[slot], off)

    def cross_copy(step, off):
        return to_peer(cross.at[step, row_place], cross_sent.at[step], cross_sem.at[step], off)

    def peer_sum(parts, slot):
        total = parts[slot, 0]
        for peer in range(1, peers):
            total = total + parts[slot, peer]
        return total

    def own(step):
        return jnp.concatenate([stay[step], moving[step]], axis=0)

    def near(step):
        return jnp.concatenate([near_stay[step], near_moving[step]], axis=0)

    stay[0] = columns[upper, :]
    moving[0] = columns[lower, :]
    stay_fac[...] = right_factor[upper, :]
    held_fac[0] = right_factor[lower, :]
    pl.semaphore_wait(barrier, 2 + peers - 1)
    moving_copy(0).start()
    stay_copy().start()
    pair = columns[...]
    start = cross_of(pair, pair)
    first[0, row_place] = start[upper]
    first[1, row_place] = start[lower]
    for off in range(1, peers):
        for slot in range(2):
            first_copy(slot, off).start()
    for off in range(1, peers):
        for slot in range(2):
            first_copy(slot, off).wait_recv()
    grams[0, upper] = peer_sum(first, 0)
    grams[0, lower] = peer_sum(first, 1)
    scale[...] = scale_of(trace(grams[0, square]))

    def rotation(step, hooks):
        gram = grams[step, square]
        twice = dot_nn(gram, gram) * scale[:1, :]
        solve[:, :order] = dot_nn(twice, twice)
        solve[:, order:] = twice
        eliminate(solve, hooks)
        turns[step] = orthogonal(solve[:, order:])

    def rotate_factor(step):
        turned = mix(turns[step], jnp.concatenate([stay_fac[...], held_fac[step]], axis=0))
        stay_fac[...] = turned[upper]
        sent_fac[step] = turned[lower]

    def advance(step, carry):
        def pass_gram():
            gram_copy(step).start()

        def products():
            moving_copy(step).wait_recv()
            cross[step, row_place] = cross_of(near_moving[step], own(step))
            for off in range(1, peers):
                cross_copy(step, off).start()

            @pl.when(step == 0)
            def _():
                stay_copy().wait_recv()
                first[2, row_place] = cross_of(near_stay[0], own(0))
                for off in range(1, peers):
                    first_copy(2, off).start()

        rotation(step, {1: pass_gram, 7: products})
        low_copy(step).start()
        top_copy(step).start()

        @pl.when(step > 0)
        def _():
            fac_copy(step - 1).wait_recv()

        turn = turns[step]
        top = turn[upper]
        top_wide = jnp.concatenate([top, jnp.zeros_like(top)], axis=0)
        stay[step + 1] = mix(top, own(step))
        rotate_factor(step)
        grams[step + 1, upper] = dot_nt(dot_nn(top, grams[step, square]), top_wide)
        fac_copy(step).start()
        low_copy(step).wait_recv()
        low = near_turns[step, lower]
        moving[step + 1] = mix(low, near(step))
        moving_copy(step + 1).start()
        top_copy(step).wait_recv()
        gram_copy(step).wait_recv()
        arrived = near_turns[step]
        low_wide = jnp.concatenate([jnp.zeros_like(low), low], axis=0)
        near_stay[step + 1] = mix(arrived[upper], near(step))
        reach = dot_nt(near_grams[step], low_wide)
        scale[...] = scale_of(trace(grams[step, square]) + trace(near_grams[step]))

        @pl.when(step == 0)
        def _():
            for off in range(1, peers):
                first_copy(2, off).wait_recv()
            grams[0, beyond] = peer_sum(first, 2)

        for off in range(1, peers):
            cross_copy(step, off).wait_recv()
        whole = jnp.concatenate([grams[step, beyond], peer_sum(cross, step)], axis=0)
        met = dot_nn(arrived, reach + dot_nt(whole, top_wide))
        grams[step + 1, beyond] = met[upper]
        grams[step + 1, lower] = met[lower]
        flipped = met.T
        across = lax.broadcasted_iota(jnp.int32, (half, order), 1)
        grams[step + 1, upper] = jnp.where(across < half, grams[step + 1, upper], flipped[upper])
        return carry

    lax.fori_loop(0, STEPS - 1, advance, 0)
    last = STEPS - 1
    rotation(last, {})
    low_copy(last).start()
    fac_copy(last - 1).wait_recv()
    rotate_factor(last)
    fac_copy(last).start()
    new_columns[upper, :] = mix(turns[last, upper], own(last))
    new_factor[upper, :] = stay_fac[...]
    moving_copy(last).wait_recv()
    low_copy(last).wait_recv()
    new_columns[lower, :] = mix(near_turns[last, lower], near(last))
    fac_copy(last).wait_recv()
    new_factor[lower, :] = held_fac[STEPS]

    stay_copy().wait_send()
    for off in range(1, peers):
        for slot in range(3):
            first_copy(slot, off).wait_send()
    for step in range(STEPS):
        moving_copy(step).wait_send()
        fac_copy(step).wait_send()
        low_copy(step).wait_send()
        if step < last:
            gram_copy(step).wait_send()
            top_copy(step).wait_send()
            for off in range(1, peers):
                cross_copy(step, off).wait_send()


def body(columns, right_factor):
    order, width = columns.shape
    half = order // 2
    fac_width = right_factor.shape[1]
    peers = lax.axis_size("rows")

    def room(*shape):
        return pltpu.VMEM(shape, jnp.float32)

    def flags(*shape):
        return pltpu.SemaphoreType.DMA(shape)

    return pl.pallas_call(
        cycle_kernel,
        out_shape=[jax.ShapeDtypeStruct(a.shape, a.dtype) for a in (columns, right_factor)],
        in_specs=[pl.BlockSpec(memory_space=pltpu.VMEM)] * 2,
        out_specs=[pl.BlockSpec(memory_space=pltpu.VMEM)] * 2,
        scratch_shapes=[
            room(STEPS, half, width),
            room(STEPS, half, width),
            room(STEPS, half, width),
            room(STEPS, half, width),
            room(half, fac_width),
            room(STEPS, half, fac_width),
            room(STEPS + 1, half, fac_width),
            room(STEPS, order + half, order),
            room(STEPS, order, order),
            room(STEPS, order, order),
            room(STEPS, order, order),
            room(3, peers, half, order),
            room(STEPS, peers, half, order),
            room(8, LANES),
            room(order, 2 * order),
            pltpu.SemaphoreType.DMA,
            pltpu.SemaphoreType.DMA,
            flags(STEPS),
            flags(STEPS),
            flags(STEPS),
            flags(STEPS),
            flags(STEPS),
            flags(STEPS),
            flags(STEPS),
            flags(STEPS),
            flags(STEPS),
            flags(STEPS),
            flags(3, peers - 1),
            flags(3, peers - 1),
            flags(STEPS, peers - 1),
            flags(STEPS, peers - 1),
        ],
        compiler_params=pltpu.CompilerParams(collective_id=0, has_side_effects=True),
        name="cycle",
    )(columns, right_factor)


def solution(mesh):
    return jax.shard_map(
        body,
        mesh=mesh,
        in_specs=(P("blk", "rows"), P("blk", "rows")),
        out_specs=(P("blk", "rows"), P("blk", "rows")),
        check_vma=False,
    )
```

time: 73.4 us -> 59.2 us (0.81)
  Pallas kernels: 70.2 us -> 56 us
    pallas_call x1, Pallas kernels: 70.2 us -> 56 us  [body(): pl.pallas_call(cycle_kernel, out_shape=[jax.ShapeDtypeStruct(a.shape, a.d...]
where the time goes in v2:
time: 59.2 us; the launch traced here: 59.1 us
  Pallas kernels  56 us (95%)
  local copies, waits for them, and re-layouts  2.41 us (4%)
  between operations  0.65 us (1%)
    pallas_call x1, Pallas kernels, body(): pl.pallas_call(cycle_kernel, out_shape=[jax.ShapeDtypeStruct(a.shape, a.d...  56 us
    unnamed x4, local copies, waits for them, and re-layouts  2.41 us

profile of v2, /device:TPU:0, one launch (start us, length us, event | category | flops | bytes accessed | tf_op | source)
XLA Modules:
  0.0 59.1 jit_solution(10849245056374309829)
XLA Ops:
  0.6 56.0 %cycle.1 = (f32[128,640]{1,0:T(8,128)}, f32[128,256]{1,0:T(8,128)}) custom-call(f32[128,640]{1,0:T(8,128)} %columns.1, f32[128,256]{1,0:T(8,128)} %right_factor.1), custom_call_target="tpu_custom_call" | custom-call | tf_op jit(solution)/shard_map/cycle/pallas_call | solution.py:354
  56.6 0.0 copy-start
  56.7 1.8 %copy.6 = f32[128,640]{1,0:T(8,128)} copy(f32[128,640]{1,0:T(8,128)} %get-tuple-element.4) | data formatting | bytes 655360
  58.4 0.0 copy-done
  58.4 0.7 %copy.7 = f32[128,256]{1,0:T(8,128)} copy(f32[128,256]{1,0:T(8,128)S(1)} %copy-done) | data formatting | bytes 262144
Async XLA Ops:
  56.6 1.8 %copy-start = (f32[128,256]{1,0:T(8,128)S(1)}, f32[128,256]{1,0:T(8,128)}, u32[]{:S(2)}) copy-start(f32[128,256]{1,0:T(8,128)} %get-tuple-element.5) | copy-start | bytes 393220

commit v3 on v2

--- a/solution.py
+++ b/solution.py
@@ -7,7 +7,10 @@
 
 STEPS = 6
 PANEL = 16
+MEET = 5
+SHARE = 6
 LANES = 128
+ROWS = 8
 MESH = pl.DeviceIdType.MESH
 
 HIGHEST_PREC = lax.Precision.HIGHEST
@@ -58,51 +61,119 @@
     )
 
 
-def eliminate(work, hooks):
+def spread_row(block, row):
+    return jnp.broadcast_to(block[row : row + 1, :], block.shape)
+
+
+def spread_lane(block, lane):
+    return jnp.broadcast_to(block[:, lane : lane + 1], (block.shape[0], LANES))
+
+
+def tree_sum(terms):
+    while len(terms) > 1:
+        terms = [sum(terms[i : i + 2][1:], terms[i]) for i in range(0, len(terms), 2)]
+    return terms[0]
+
+
+def eliminate(work, unit, hooks):
     order, width = work.shape
     panels = order // PANEL
+    one = unit[...]
+    wide_one = jnp.concatenate([one, one], axis=0)
+    ahead = work[:PANEL, :]
+    tiles = range(width // LANES)
+    down = lax.broadcasted_iota(jnp.int32, (ROWS, LANES), 0)
+
+    def part(block, group, t):
+        return block[group * ROWS : (group + 1) * ROWS, t * LANES : (t + 1) * LANES]
+
     for panel in range(panels):
         if panel in hooks:
             hooks[panel]()
         low = panel * PANEL
         high = low + PANEL
         end = min(high + PANEL, order)
-        rows = work[low:high, :]
-        below = work[high:end, :] if end > high else None
-        spread = [
-            jnp.broadcast_to(rows[:, low + k : low + k + 1], (PANEL, 128)) for k in range(PANEL)
+        own = ahead
+        rows = [[part(own, g, t) for t in tiles] for g in range(2)]
+        result = [rows[0][1], rows[1][1]]
+        first_heads, second_heads = [], []
+        for k in range(ROWS):
+            both = spread_lane(own[:, :LANES], low + k) * wide_one
+            first_heads.append(both[:ROWS])
+            second_heads.append(both[ROWS:])
+        for k in range(ROWS, PANEL):
+            second_heads.append(spread_lane(rows[1][0], low + k) * one)
+        scales = [jnp.zeros((ROWS, LANES), jnp.float32) for g in range(2)]
+        pivot = spread_row(first_heads[0], 0)
+        for j in range(ROWS):
+            root = lax.rsqrt(pivot)
+            inverse = root * root
+            if j + 1 < ROWS:
+                side = spread_row(first_heads[j], j + 1) * root
+                pivot = spread_row(first_heads[j + 1], j + 1) - side * side
+            else:
+                side = spread_row(second_heads[j], 0) * root
+                pivot = spread_row(second_heads[j + 1], 0) - side * side
+            column = [first_heads[j] * inverse, second_heads[j] * inverse]
+            onward = jnp.where(down > j, column[0], 0.0)
+            column[0] = jnp.where(down == j, 1.0 - inverse, column[0])
+            scales[0] = jnp.where(down == j, root, scales[0])
+            front = [spread_row(rows[0][t], j) for t in tiles]
+            rows = [[rows[g][t] - column[g] * front[t] for t in tiles] for g in range(2)]
+            front = spread_row(result[0], j)
+            result = [result[0] - onward * front, result[1] - column[1] * front]
+            for k in range(j + 1, ROWS):
+                head = spread_row(first_heads[k], j)
+                first_heads[k] = first_heads[k] - column[0] * head
+                second_heads[k] = second_heads[k] - column[1] * head
+            for k in range(ROWS, PANEL):
+                head = spread_row(second_heads[j], k - ROWS)
+                second_heads[k] = second_heads[k] - column[1] * head
+        above = [spread_lane(rows[0][0], low + k) for k in range(ROWS, PANEL)]
+        for j in range(ROWS, PANEL):
+            row = j - ROWS
+            root = lax.rsqrt(pivot)
+            inverse = root * root
+            if j + 1 < PANEL:
+                side = spread_row(second_heads[j], row + 1) * root
+                pivot = spread_row(second_heads[j + 1], row + 1) - side * side
+            column = second_heads[j] * inverse
+            onward = jnp.where(down > row, column, 0.0)
+            column = jnp.where(down == row, 1.0 - inverse, column)
+            scales[1] = jnp.where(down == row, root, scales[1])
+            rows[1] = [rows[1][t] - column * spread_row(rows[1][t], row) for t in tiles]
+            result[1] = result[1] - onward * spread_row(result[1], row)
+            for k in range(j + 1, PANEL):
+                second_heads[k] = second_heads[k] - column * spread_row(second_heads[k], row)
+        for g in range(2):
+            start = low + g * ROWS
+            work[start : start + ROWS, LANES:] = result[g] * scales[g]
+        if end == high:
+            continue
+        fronts = [[spread_row(rows[1][t], k) for t in tiles] for k in range(ROWS)]
+        rows[0] = [
+            rows[0][t] - tree_sum([above[k] * fronts[k][t] for k in range(ROWS)]) for t in tiles
         ]
-        spread_below = None
-        if below is not None:
-            spread_below = [
-                jnp.broadcast_to(below[:, low + k : low + k + 1], (end - high, 128))
-                for k in range(PANEL)
+        fronts = [[spread_row(rows[0][t], k) for t in tiles] for k in range(ROWS)] + fronts
+        below = work[high:end, :]
+        heads = [spread_lane(below[:, :LANES], low + k) for k in range(PANEL)]
+        ahead = []
+        for g in range(2):
+            moved = [
+                tree_sum([part(heads[k], g, 0) * fronts[k][t] for k in range(PANEL)]) for t in tiles
             ]
-        done = []
-        for j in range(PANEL):
-            scale = lax.rsqrt(spread[j][j : j + 1, :])
-            column = spread[j] * scale
-            wide = jnp.concatenate([scale] * (width // 128), axis=1)
-            pivot_row = rows[j : j + 1, :] * wide
-            done.append(pivot_row)
-            wide_column = jnp.concatenate([column] * (width // 128), axis=1)
-            if j + 1 < PANEL:
-                rows = rows - wide_column * pivot_row
-            if below is not None:
-                column_below = spread_below[j] * scale
-                wide_below = jnp.concatenate([column_below] * (width // 128), axis=1)
-                below = below - wide_below * pivot_row
-            for k in range(j + 1, PANEL):
-                head = spread[k][j : j + 1, :] * scale
-                spread[k] = spread[k] - column * head
-                if below is not None:
-                    spread_below[k] = spread_below[k] - column_below * head
-        finished = jnp.concatenate(done, axis=0)
-        work[low:high, :] = finished
-        if below is not None:
-            work[high:end, :] = below
+            ahead.append(jnp.concatenate([part(below, g, t) - moved[t] for t in tiles], axis=1))
+        ahead = jnp.concatenate(ahead, axis=0)
         if end < order:
-            work[end:, :] = work[end:, :] - dot_tn(finished[:, end:order], finished)
+            solved = jnp.concatenate([jnp.concatenate(rows[g], axis=1) for g in range(2)], axis=0)
+            work[end:, :] = work[end:, :] - trailing(work, low, high, end, solved)
+
+
+def trailing(work, low, high, end, solved):
+    order = work.shape[0]
+    parts = [jnp.zeros((low, solved.shape[1]), jnp.float32)] if low else []
+    parts += [solved, jnp.zeros((order - high, solved.shape[1]), jnp.float32)]
+    return dot_nn(work[end:, :order], jnp.concatenate(parts, axis=0))
 
 
 def grid_of(shape):
@@ -124,12 +195,12 @@
     down, across = grid_of(overlap.shape)
     lower = jnp.where(down > across, overlap, 0.0)
     lower = jnp.where(down == across, 0.5 * (overlap - 1.0), lower)
-    return turn - dot_nn(lower, turn)
+    return turn - mix(lower, turn)
 
 
 def cycle_kernel(
     columns, right_factor, new_columns, new_factor, stay, moving, near_stay, near_moving, stay_fac, sent_fac,
-    held_fac, grams, near_grams, turns, near_turns, first, cross, scale, solve, stay_sent,
+    held_fac, grams, near_grams, turns, near_turns, first, cross, reach, reach_across, scale, unit, solve, stay_sent,
     stay_sem, moving_sent, moving_sem, fac_sent, fac_sem, gram_sent, gram_sem, low_sent, low_sem, top_sent,
     top_sem, first_sent, first_sem, cross_sent, cross_sem,
 ):
@@ -173,7 +244,7 @@
 
     def gram_copy(step):
         return to_right(
-            grams.at[step, square], near_grams.at[step], gram_sent.at[step], gram_sem.at[step]
+            grams.at[step], near_grams.at[step], gram_sent.at[step], gram_sem.at[step]
         )
 
     def low_copy(step):
@@ -214,6 +285,7 @@
     def near(step):
         return jnp.concatenate([near_stay[step], near_moving[step]], axis=0)
 
+    unit[...] = jnp.ones_like(unit)
     stay[0] = columns[upper, :]
     moving[0] = columns[lower, :]
     stay_fac[...] = right_factor[upper, :]
@@ -233,92 +305,106 @@
             first_copy(slot, off).wait_recv()
     grams[0, upper] = peer_sum(first, 0)
     grams[0, lower] = peer_sum(first, 1)
-    scale[...] = scale_of(trace(grams[0, square]))
+    scale[...] = scale_of(trace(grams[0]))
 
     def rotation(step, hooks):
-        gram = grams[step, square]
+        gram = grams[step]
         twice = dot_nn(gram, gram) * scale[:1, :]
         solve[:, :order] = dot_nn(twice, twice)
         solve[:, order:] = twice
-        eliminate(solve, hooks)
-        turns[step] = orthogonal(solve[:, order:])
+        eliminate(solve, unit, hooks)
+        if order // PANEL in hooks:
+            hooks[order // PANEL]()
+        turns[step, square] = orthogonal(solve[:, order:])
+        low_copy(step).start()
 
     def rotate_factor(step):
-        turned = mix(turns[step], jnp.concatenate([stay_fac[...], held_fac[step]], axis=0))
+        turned = mix(turns[step, square], jnp.concatenate([stay_fac[...], held_fac[step]], axis=0))
         stay_fac[...] = turned[upper]
         sent_fac[step] = turned[lower]
 
+    def meet(step):
+        moving_copy(step).wait_recv()
+        cross[step, row_place] = cross_of(near_moving[step], own(step))
+
+    def share(step):
+        for off in range(1, peers):
+            cross_copy(step, off).start()
+
+    def meet_first():
+        meet(0)
+        stay_copy().wait_recv()
+        first[2, row_place] = cross_of(near_stay[0], own(0))
+
+    def share_first():
+        share(0)
+        for off in range(1, peers):
+            first_copy(2, off).start()
+
+    last = STEPS - 1
+    gram_copy(0).start()
+    rotation(0, {MEET: meet_first, SHARE: share_first})
+    top_copy(0).start()
+    for off in range(1, peers):
+        first_copy(2, off).wait_recv()
+    turns[0, beyond] = peer_sum(first, 2)
+
     def advance(step, carry):
-        def pass_gram():
-            gram_copy(step).start()
-
-        def products():
-            moving_copy(step).wait_recv()
-            cross[step, row_place] = cross_of(near_moving[step], own(step))
-            for off in range(1, peers):
-                cross_copy(step, off).start()
-
-            @pl.when(step == 0)
-            def _():
-                stay_copy().wait_recv()
-                first[2, row_place] = cross_of(near_stay[0], own(0))
-                for off in range(1, peers):
-                    first_copy(2, off).start()
-
-        rotation(step, {1: pass_gram, 7: products})
-        low_copy(step).start()
-        top_copy(step).start()
+        then = step + 1
+        top = turns[step, upper]
+        top_wide = jnp.concatenate([top, jnp.zeros_like(top)], axis=0)
+        grams[then, upper] = dot_nt(dot_nn(top, grams[step]), top_wide)
+        stay[then] = mix(top, own(step))
 
         @pl.when(step > 0)
         def _():
             fac_copy(step - 1).wait_recv()
 
-        turn = turns[step]
-        top = turn[upper]
-        top_wide = jnp.concatenate([top, jnp.zeros_like(top)], axis=0)
-        stay[step + 1] = mix(top, own(step))
         rotate_factor(step)
-        grams[step + 1, upper] = dot_nt(dot_nn(top, grams[step, square]), top_wide)
         fac_copy(step).start()
+        gram_copy(step).wait_recv()
+        scale[...] = scale_of(trace(grams[step]) + trace(near_grams[step]))
+        for off in range(1, peers):
+            cross_copy(step, off).wait_recv()
+        whole = jnp.concatenate([turns[step, beyond], peer_sum(cross, step)], axis=0)
+        reach[...] = dot_nt(whole, top_wide)
+        reach_across[...] = dot_nt(top, whole)
         low_copy(step).wait_recv()
         low = near_turns[step, lower]
-        moving[step + 1] = mix(low, near(step))
-        moving_copy(step + 1).start()
+        moving[then] = mix(low, near(step))
+        moving_copy(then).start()
+        low_wide = jnp.concatenate([jnp.zeros_like(low), low], axis=0)
+        reach[...] += dot_nt(near_grams[step], low_wide)
+        grams[then, upper] += dot_nt(reach_across[...], low_wide)
+        grams[then, lower] = dot_nn(low, reach[...])
+
+        @pl.when(then < last)
+        def _():
+            gram_copy(then).start()
+
+        def share_then():
+            @pl.when(then < last)
+            def _():
+                share(then)
+
+        rotation(then, {MEET: lambda: meet(then), SHARE: share_then})
+
+        @pl.when(then < last)
+        def _():
+            top_copy(then).start()
+
         top_copy(step).wait_recv()
-        gram_copy(step).wait_recv()
-        arrived = near_turns[step]
-        low_wide = jnp.concatenate([jnp.zeros_like(low), low], axis=0)
-        near_stay[step + 1] = mix(arrived[upper], near(step))
-        reach = dot_nt(near_grams[step], low_wide)
-        scale[...] = scale_of(trace(grams[step, square]) + trace(near_grams[step]))
-
-        @pl.when(step == 0)
-        def _():
-            for off in range(1, peers):
-                first_copy(2, off).wait_recv()
-            grams[0, beyond] = peer_sum(first, 2)
-
-        for off in range(1, peers):
-            cross_copy(step, off).wait_recv()
-        whole = jnp.concatenate([grams[step, beyond], peer_sum(cross, step)], axis=0)
-        met = dot_nn(arrived, reach + dot_nt(whole, top_wide))
-        grams[step + 1, beyond] = met[upper]
-        grams[step + 1, lower] = met[lower]
-        flipped = met.T
-        across = lax.broadcasted_iota(jnp.int32, (half, order), 1)
-        grams[step + 1, upper] = jnp.where(across < half, grams[step + 1, upper], flipped[upper])
+        arrived = near_turns[step, upper]
+        near_stay[then] = mix(arrived, near(step))
+        turns[then, beyond] = dot_nn(arrived, reach[...])
         return carry
 
-    lax.fori_loop(0, STEPS - 1, advance, 0)
-    last = STEPS - 1
-    rotation(last, {})
-    low_copy(last).start()
+    lax.fori_loop(0, last, advance, 0)
     fac_copy(last - 1).wait_recv()
     rotate_factor(last)
     fac_copy(last).start()
     new_columns[upper, :] = mix(turns[last, upper], own(last))
     new_factor[upper, :] = stay_fac[...]
-    moving_copy(last).wait_recv()
     low_copy(last).wait_recv()
     new_columns[lower, :] = mix(near_turns[last, lower], near(last))
     fac_copy(last).wait_recv()
@@ -364,12 +450,15 @@
             room(half, fac_width),
             room(STEPS, half, fac_width),
             room(STEPS + 1, half, fac_width),
-            room(STEPS, order + half, order),
             room(STEPS, order, order),
             room(STEPS, order, order),
+            room(STEPS, order + half, order),
             room(STEPS, order, order),
             room(3, peers, half, order),
             room(STEPS, peers, half, order),
+            room(order, order),
+            room(half, order),
+            room(8, LANES),
             room(8, LANES),
             room(order, 2 * order),
             pltpu.SemaphoreType.DMA,
@@ -389,7 +478,9 @@
             flags(STEPS, peers - 1),
             flags(STEPS, peers - 1),
         ],
-        compiler_params=pltpu.CompilerParams(collective_id=0, has_side_effects=True),
+        compiler_params=pltpu.CompilerParams(
+            collective_id=0, has_side_effects=True, vmem_limit_bytes=24 * 1024 * 1024
+        ),
         name="cycle",
     )(columns, right_factor)
 

time: 59.2 us -> 55.7 us (0.941)
  Pallas kernels: 56 us -> 51.6 us
  local copies, waits for them, and re-layouts: 2.41 us -> 3.25 us
    pallas_call x1, Pallas kernels: 56 us -> 51.6 us  [body(): pl.pallas_call(cycle_kernel, out_shape=[jax.ShapeDtypeStruct(a.shape, a.d...]
    unnamed x4 -> x6, local copies, waits for them, and re-layouts: 2.41 us -> 3.25 us
where the time goes in v3:
time: 55.7 us; the launch traced here: 55.5 us
  Pallas kernels  51.6 us (93%)
  local copies, waits for them, and re-layouts  3.25 us (6%)
  between operations  0.65 us (1%)
    pallas_call x1, Pallas kernels, body(): pl.pallas_call(cycle_kernel, out_shape=[jax.ShapeDtypeStruct(a.shape, a.d...  51.6 us
    unnamed x6, local copies, waits for them, and re-layouts  3.25 us

profile of v3, /device:TPU:0, one launch (start us, length us, event | category | flops | bytes accessed | tf_op | source)
XLA Modules:
  0.0 55.5 jit_solution(10787277242458657413)
XLA Ops:
  0.6 0.0 copy-start
  0.6 1.0 %copy-done = f32[128,640]{1,0:T(8,128)S(1)} copy-done((f32[128,640]{1,0:T(8,128)S(1)}, f32[128,640]{1,0:T(8,128)}, u32[]{:S(2)}) %copy-start) | copy-done | bytes 327704
  1.6 0.0 copy-start.1
  1.6 0.9 %copy-done.1 = f32[128,256]{1,0:T(8,128)S(1)} copy-done((f32[128,256]{1,0:T(8,128)S(1)}, f32[128,256]{1,0:T(8,128)}, u32[]{:S(2)}) %copy-start.1) | copy-done | bytes 131096
  2.5 51.6 %cycle.1 = (f32[128,640]{1,0:T(8,128)S(1)}, f32[128,256]{1,0:T(8,128)S(1)}) custom-call(f32[128,640]{1,0:T(8,128)S(1)} %copy-done, f32[128,256]{1,0:T(8,128)S(1)} %copy-done.1), custom_call_target="tpu_custom_call" | custom-call | tf_op jit(solution)/shard_map/cycle/pallas_call | solution.py:440
  54.2 0.7 %copy.6 = f32[128,640]{1,0:T(8,128)} copy(f32[128,640]{1,0:T(8,128)S(1)} %get-tuple-element.4) | data formatting | bytes 655360
  54.9 0.7 %copy.7 = f32[128,256]{1,0:T(8,128)} copy(f32[128,256]{1,0:T(8,128)S(1)} %get-tuple-element.5) | data formatting | bytes 262144
Async XLA Ops:
  0.6 1.0 %copy-start = (f32[128,640]{1,0:T(8,128)S(1)}, f32[128,640]{1,0:T(8,128)}, u32[]{:S(2)}) copy-start(f32[128,640]{1,0:T(8,128)} %columns.1) | copy-start | bytes 983044
  1.6 0.9 %copy-start.1 = (f32[128,256]{1,0:T(8,128)S(1)}, f32[128,256]{1,0:T(8,128)}, u32[]{:S(2)}) copy-start(f32[128,256]{1,0:T(8,128)} %right_factor.1) | copy-start | bytes 393220

commit v4 on v3

--- a/solution.py
+++ b/solution.py
@@ -47,6 +47,35 @@
 def split_right(b, axis=0):
     high, low = split(b)
     return jnp.concatenate([high, high, low], axis=axis)
+
+
+def split_three(a):
+    high = a.astype(jnp.bfloat16)
+    rest = a - high.astype(jnp.float32)
+    mid = rest.astype(jnp.bfloat16)
+    return high, mid, (rest - mid.astype(jnp.float32)).astype(jnp.bfloat16)
+
+
+def six_left(a):
+    high, mid, low = split_three(a)
+    return jnp.concatenate([low, high, mid, mid, high, high], axis=1)
+
+
+def six_right(b, axis):
+    high, mid, low = split_three(b)
+    return jnp.concatenate([high, low, mid, high, mid, high], axis=axis)
+
+
+def six_nn(a, b):
+    return lax.dot_general(
+        six_left(a), six_right(b, 0), (((1,), (0,)), ((), ())), preferred_element_type=jnp.float32
+    )
+
+
+def six_nt(a, b):
+    return lax.dot_general(
+        six_left(a), six_right(b, 1), (((1,), (1,)), ((), ())), preferred_element_type=jnp.float32
+    )
 
 
 def mix(turn, block):
@@ -191,7 +220,7 @@
 
 
 def orthogonal(turn):
-    overlap = dot_nt(turn, turn)
+    overlap = six_nt(turn, turn)
     down, across = grid_of(overlap.shape)
     lower = jnp.where(down > across, overlap, 0.0)
     lower = jnp.where(down == across, 0.5 * (overlap - 1.0), lower)
@@ -309,8 +338,8 @@
 
     def rotation(step, hooks):
         gram = grams[step]
-        twice = dot_nn(gram, gram) * scale[:1, :]
-        solve[:, :order] = dot_nn(twice, twice)
+        twice = six_nn(gram, gram) * scale[:1, :]
+        solve[:, :order] = six_nn(twice, twice)
         solve[:, order:] = twice
         eliminate(solve, unit, hooks)
         if order // PANEL in hooks:
@@ -353,7 +382,7 @@
         then = step + 1
         top = turns[step, upper]
         top_wide = jnp.concatenate([top, jnp.zeros_like(top)], axis=0)
-        grams[then, upper] = dot_nt(dot_nn(top, grams[step]), top_wide)
+        grams[then, upper] = six_nt(six_nn(top, grams[step]), top_wide)
         stay[then] = mix(top, own(step))
 
         @pl.when(step > 0)
@@ -367,16 +396,16 @@
         for off in range(1, peers):
             cross_copy(step, off).wait_recv()
         whole = jnp.concatenate([turns[step, beyond], peer_sum(cross, step)], axis=0)
-        reach[...] = dot_nt(whole, top_wide)
-        reach_across[...] = dot_nt(top, whole)
+        reach[...] = six_nt(whole, top_wide)
+        reach_across[...] = six_nt(top, whole)
         low_copy(step).wait_recv()
         low = near_turns[step, lower]
         moving[then] = mix(low, near(step))
         moving_copy(then).start()
         low_wide = jnp.concatenate([jnp.zeros_like(low), low], axis=0)
-        reach[...] += dot_nt(near_grams[step], low_wide)
-        grams[then, upper] += dot_nt(reach_across[...], low_wide)
-        grams[then, lower] = dot_nn(low, reach[...])
+        reach[...] += six_nt(near_grams[step], low_wide)
+        grams[then, upper] += six_nt(reach_across[...], low_wide)
+        grams[then, lower] = six_nn(low, reach[...])
 
         @pl.when(then < last)
         def _():

time: 55.7 us -> 54.8 us (0.984)
  Pallas kernels: 51.6 us -> 50.8 us
    pallas_call x1, Pallas kernels: 51.6 us -> 50.8 us  [body(): pl.pallas_call(cycle_kernel, out_shape=[jax.ShapeDtypeStruct(a.shape, a.d...]
where the time goes in v4:
time: 54.8 us; the launch traced here: 54.7 us
  Pallas kernels  50.8 us (93%)
  local copies, waits for them, and re-layouts  3.25 us (6%)
  between operations  0.65 us (1%)
    pallas_call x1, Pallas kernels, body(): pl.pallas_call(cycle_kernel, out_shape=[jax.ShapeDtypeStruct(a.shape, a.d...  50.8 us
    unnamed x6, local copies, waits for them, and re-layouts  3.25 us

profile of v4, /device:TPU:0, one launch (start us, length us, event | category | flops | bytes accessed | tf_op | source)
XLA Modules:
  0.0 54.7 jit_solution(2619851821965701388)
XLA Ops:
  0.6 0.0 copy-start
  0.6 1.0 %copy-done = f32[128,640]{1,0:T(8,128)S(1)} copy-done((f32[128,640]{1,0:T(8,128)S(1)}, f32[128,640]{1,0:T(8,128)}, u32[]{:S(2)}) %copy-start) | copy-done | bytes 327704
  1.6 0.0 copy-start.1
  1.6 0.9 %copy-done.1 = f32[128,256]{1,0:T(8,128)S(1)} copy-done((f32[128,256]{1,0:T(8,128)S(1)}, f32[128,256]{1,0:T(8,128)}, u32[]{:S(2)}) %copy-start.1) | copy-done | bytes 131096
  2.5 50.8 %cycle.1 = (f32[128,640]{1,0:T(8,128)S(1)}, f32[128,256]{1,0:T(8,128)S(1)}) custom-call(f32[128,640]{1,0:T(8,128)S(1)} %copy-done, f32[128,256]{1,0:T(8,128)S(1)} %copy-done.1), custom_call_target="tpu_custom_call" | custom-call | tf_op jit(solution)/shard_map/cycle/pallas_call | solution.py:469
  53.3 0.7 %copy.6 = f32[128,640]{1,0:T(8,128)} copy(f32[128,640]{1,0:T(8,128)S(1)} %get-tuple-element.4) | data formatting | bytes 655360
  54.0 0.7 %copy.7 = f32[128,256]{1,0:T(8,128)} copy(f32[128,256]{1,0:T(8,128)S(1)} %get-tuple-element.5) | data formatting | bytes 262144
Async XLA Ops:
  0.6 1.0 %copy-start = (f32[128,640]{1,0:T(8,128)S(1)}, f32[128,640]{1,0:T(8,128)}, u32[]{:S(2)}) copy-start(f32[128,640]{1,0:T(8,128)} %columns.1) | copy-start | bytes 983044
  1.6 0.9 %copy-start.1 = (f32[128,256]{1,0:T(8,128)S(1)}, f32[128,256]{1,0:T(8,128)}, u32[]{:S(2)}) copy-start(f32[128,256]{1,0:T(8,128)} %right_factor.1) | copy-start | bytes 393220

commit v5 on v4

--- a/solution.py
+++ b/solution.py
@@ -374,6 +374,8 @@
     gram_copy(0).start()
     rotation(0, {MEET: meet_first, SHARE: share_first})
     top_copy(0).start()
+    rotate_factor(0)
+    fac_copy(0).start()
     for off in range(1, peers):
         first_copy(2, off).wait_recv()
     turns[0, beyond] = peer_sum(first, 2)
@@ -385,12 +387,6 @@
         grams[then, upper] = six_nt(six_nn(top, grams[step]), top_wide)
         stay[then] = mix(top, own(step))
 
-        @pl.when(step > 0)
-        def _():
-            fac_copy(step - 1).wait_recv()
-
-        rotate_factor(step)
-        fac_copy(step).start()
         gram_copy(step).wait_recv()
         scale[...] = scale_of(trace(grams[step]) + trace(near_grams[step]))
         for off in range(1, peers):
@@ -422,6 +418,9 @@
         def _():
             top_copy(then).start()
 
+        fac_copy(step).wait_recv()
+        rotate_factor(then)
+        fac_copy(then).start()
         top_copy(step).wait_recv()
         arrived = near_turns[step, upper]
         near_stay[then] = mix(arrived, near(step))
@@ -429,9 +428,6 @@
         return carry
 
     lax.fori_loop(0, last, advance, 0)
-    fac_copy(last - 1).wait_recv()
-    rotate_factor(last)
-    fac_copy(last).start()
     new_columns[upper, :] = mix(turns[last, upper], own(last))
     new_factor[upper, :] = stay_fac[...]
     low_copy(last).wait_recv()

time: 54.8 us -> 54.3 us (level)
  Pallas kernels: 50.8 us -> 50.2 us
    pallas_call x1, Pallas kernels: 50.8 us -> 50.2 us  [body(): pl.pallas_call(cycle_kernel, out_shape=[jax.ShapeDtypeStruct(a.shape, a.d...]
where the time goes in v5:
time: 54.3 us; the launch traced here: 54.1 us
  Pallas kernels  50.2 us (92%)
  local copies, waits for them, and re-layouts  3.25 us (6%)
  between operations  0.65 us (1%)
    pallas_call x1, Pallas kernels, body(): pl.pallas_call(cycle_kernel, out_shape=[jax.ShapeDtypeStruct(a.shape, a.d...  50.2 us
    unnamed x6, local copies, waits for them, and re-layouts  3.25 us

profile of v5, /device:TPU:0, one launch (start us, length us, event | category | flops | bytes accessed | tf_op | source)
XLA Modules:
  0.0 54.1 jit_solution(4360839269834377813)
XLA Ops:
  0.6 0.0 copy-start
  0.6 1.0 %copy-done = f32[128,640]{1,0:T(8,128)S(1)} copy-done((f32[128,640]{1,0:T(8,128)S(1)}, f32[128,640]{1,0:T(8,128)}, u32[]{:S(2)}) %copy-start) | copy-done | bytes 327704
  1.6 0.0 copy-start.1
  1.6 0.9 %copy-done.1 = f32[128,256]{1,0:T(8,128)S(1)} copy-done((f32[128,256]{1,0:T(8,128)S(1)}, f32[128,256]{1,0:T(8,128)}, u32[]{:S(2)}) %copy-start.1) | copy-done | bytes 131096
  2.5 50.2 %cycle.1 = (f32[128,640]{1,0:T(8,128)S(1)}, f32[128,256]{1,0:T(8,128)S(1)}) custom-call(f32[128,640]{1,0:T(8,128)S(1)} %copy-done, f32[128,256]{1,0:T(8,128)S(1)} %copy-done.1), custom_call_target="tpu_custom_call" | custom-call | tf_op jit(solution)/shard_map/cycle/pallas_call | solution.py:465
  52.7 0.7 %copy.6 = f32[128,640]{1,0:T(8,128)} copy(f32[128,640]{1,0:T(8,128)S(1)} %get-tuple-element.4) | data formatting | bytes 655360
  53.4 0.7 %copy.7 = f32[128,256]{1,0:T(8,128)} copy(f32[128,256]{1,0:T(8,128)S(1)} %get-tuple-element.5) | data formatting | bytes 262144
Async XLA Ops:
  0.6 1.0 %copy-start = (f32[128,640]{1,0:T(8,128)S(1)}, f32[128,640]{1,0:T(8,128)}, u32[]{:S(2)}) copy-start(f32[128,640]{1,0:T(8,128)} %columns.1) | copy-start | bytes 983044
  1.6 0.9 %copy-start.1 = (f32[128,256]{1,0:T(8,128)S(1)}, f32[128,256]{1,0:T(8,128)}, u32[]{:S(2)}) copy-start(f32[128,256]{1,0:T(8,128)} %right_factor.1) | copy-start | bytes 393220

commit v6 on v5

--- a/solution.py
+++ b/solution.py
@@ -424,7 +424,7 @@
         top_copy(step).wait_recv()
         arrived = near_turns[step, upper]
         near_stay[then] = mix(arrived, near(step))
-        turns[then, beyond] = dot_nn(arrived, reach[...])
+        turns[then, beyond] = six_nn(arrived, reach[...])
         return carry
 
     lax.fori_loop(0, last, advance, 0)

time: 54.3 us -> 54.2 us (level)
  no operation moved by 1% of the time
where the time goes in v6:
time: 54.2 us; the launch traced here: 54 us
  Pallas kernels  50.1 us (92%)
  local copies, waits for them, and re-layouts  3.25 us (6%)
  between operations  0.65 us (1%)
    pallas_call x1, Pallas kernels, body(): pl.pallas_call(cycle_kernel, out_shape=[jax.ShapeDtypeStruct(a.shape, a.d...  50.1 us
    unnamed x6, local copies, waits for them, and re-layouts  3.25 us

profile of v6, /device:TPU:0, one launch (start us, length us, event | category | flops | bytes accessed | tf_op | source)
XLA Modules:
  0.0 54.0 jit_solution(2503877642789261238)
XLA Ops:
  0.6 0.0 copy-start
  0.6 1.0 %copy-done = f32[128,640]{1,0:T(8,128)S(1)} copy-done((f32[128,640]{1,0:T(8,128)S(1)}, f32[128,640]{1,0:T(8,128)}, u32[]{:S(2)}) %copy-start) | copy-done | bytes 327704
  1.6 0.0 copy-start.1
  1.6 0.9 %copy-done.1 = f32[128,256]{1,0:T(8,128)S(1)} copy-done((f32[128,256]{1,0:T(8,128)S(1)}, f32[128,256]{1,0:T(8,128)}, u32[]{:S(2)}) %copy-start.1) | copy-done | bytes 131096
  2.5 50.1 %cycle.1 = (f32[128,640]{1,0:T(8,128)S(1)}, f32[128,256]{1,0:T(8,128)S(1)}) custom-call(f32[128,640]{1,0:T(8,128)S(1)} %copy-done, f32[128,256]{1,0:T(8,128)S(1)} %copy-done.1), custom_call_target="tpu_custom_call" | custom-call | tf_op jit(solution)/shard_map/cycle/pallas_call | solution.py:465
  52.7 0.7 %copy.6 = f32[128,640]{1,0:T(8,128)} copy(f32[128,640]{1,0:T(8,128)S(1)} %get-tuple-element.4) | data formatting | bytes 655360
  53.4 0.7 %copy.7 = f32[128,256]{1,0:T(8,128)} copy(f32[128,256]{1,0:T(8,128)S(1)} %get-tuple-element.5) | data formatting | bytes 262144
Async XLA Ops:
  0.6 1.0 %copy-start = (f32[128,640]{1,0:T(8,128)S(1)}, f32[128,640]{1,0:T(8,128)}, u32[]{:S(2)}) copy-start(f32[128,640]{1,0:T(8,128)} %columns.1) | copy-start | bytes 983044
  1.6 0.9 %copy-start.1 = (f32[128,256]{1,0:T(8,128)S(1)}, f32[128,256]{1,0:T(8,128)}, u32[]{:S(2)}) copy-start(f32[128,256]{1,0:T(8,128)} %right_factor.1) | copy-start | bytes 393220
